TPU v7x, 32 devices: a whole 2x2x4 slice. The times are simulated.
32 devices in a mesh: samp: 4 (over z), atom: 8 (over y, x, core).
Axes of the slice: x: 2, y: 2, z: 4, core: 2. Of those that a mesh axis runs over, the one named last changes fastest.
Arguments:
- atom_state: bfloat16 [16, 2560, 128], P('samp', 'atom'), may hold values from -6 to 6, as said below
- atom_token: int32 [2560], P('atom'), may hold values from 0 to 319, never falling along the last dimension, each value on 1 to 24 neighbouring positions
- window_valid: int32 [80], P('atom'), may hold values from 1 to 32
- attend_gain: float32 [128], replicated, may hold values from 0.25 to 1.75
- project_weight: bfloat16 [128, 384], replicated, may hold values from -4 to 4
- output_weight: bfloat16 [128, 128], replicated, may hold values from -1.5 to 1.5
- token_bias: float32 [4], replicated, may hold values from -2 to 2
- transit_gain: float32 [128], replicated, may hold values from 0.25 to 1.75
- transit_weight: bfloat16 [128, 512], replicated, may hold values from -0.5 to 0.5
- return_weight: bfloat16 [256, 128], replicated, may hold values from -0.375 to 0.375
- cotangent: bfloat16 [16, 2560, 128], P('samp', 'atom'), may hold values from -6 to 6
Outputs:
- block_out: bfloat16 [16, 2560, 128], P('samp', 'atom')
- state_grad: bfloat16 [16, 2560, 128], P('samp', 'atom')
- grad_attend_gain: float32 [128], replicated
- grad_project: float32 [128, 384], replicated
- grad_output: float32 [128, 128], replicated
- grad_bias: float32 [4], replicated
- grad_transit_gain: float32 [128], replicated
- grad_transit: float32 [128, 512], replicated
- grad_return: float32 [256, 128], replicated
Inputs may be any that keep to these rules, and one draw needn't show every extreme that they name: atom_state is finite. `atom_token`: tokens are numbered in order along the atoms; a token has 1 to 24 atoms.
All inputs are finite; a program needn't handle non-finite values.
Results may differ from a plain program's by a relative error of at most 0.025.
The roundings to bfloat16 on the way count: a program that leaves them out, or rounds other values in their place, can miss the bound.
Values may be sent and summed in bfloat16 or wider, within the bound.
A program may use at most 64 MiB of HBM per device.

v0:
```python
import jax
import jax.numpy as jnp
from jax import lax
from jax.sharding import PartitionSpec as P

HEADS = 4
TRANS = 256
QWIN = 32
KWIN = 128
HALO = 48


PRECISE = lax.Precision.HIGHEST
EPSILON = 1e-05
CLIP_NORM = 256.0


def with_halo(value, sides, width):
    for axis, dim in sides:
        size, length = (lax.axis_size(axis), value.shape[dim])
        up = [(i, (i + 1) % size) for i in range(size - 1)]
        down = [(j, i) for i, j in up]
        last = lax.slice_in_dim(value, length - width, length, axis=dim)
        first = lax.slice_in_dim(value, 0, width, axis=dim)
        before = lax.ppermute(last, axis, up)
        after = lax.ppermute(first, axis, down)
        value = jnp.concatenate([before, value, after], axis=dim)
    return value


def passed_along(value, axis, by):
    size = lax.axis_size(axis)
    pairs = [(i, i + by) for i in range(size) if 0 <= i + by < size]
    return lax.ppermute(value, axis, pairs)


def normalize(values, scaling):
    values = values.astype(jnp.float32)
    center = jnp.mean(values, axis=-1, keepdims=True)
    shifted = values - center
    variance = jnp.mean(shifted * shifted, axis=-1, keepdims=True)
    return shifted * lax.rsqrt(variance + EPSILON) * scaling


def token_codes(atom_token, window_valid):
    windows_here = window_valid.shape[0]
    slots = lax.broadcasted_iota(jnp.int32, (windows_here, QWIN), 1)
    inside = (slots < window_valid[:, None]).reshape(-1)
    return jnp.where(inside, atom_token + 1, 0)


def attend(queries, pairs, query_ids, ext_ids, token_bias):
    channels = queries.shape[1]
    window_count = queries.shape[0] // QWIN
    extra_blocks = 2 * HALO // QWIN
    span_blocks = KWIN // QWIN
    head_dim = channels // HEADS
    blocks = pairs.reshape(window_count + extra_blocks, QWIN, 2 * channels)
    gathered = jnp.concatenate(
        [blocks[offset : offset + window_count] for offset in range(span_blocks)], axis=1
    )
    code_blocks = ext_ids.reshape(window_count + extra_blocks, QWIN)
    key_ids = jnp.concatenate(
        [code_blocks[offset : offset + window_count] for offset in range(span_blocks)], axis=1
    )
    query_blocks = queries.reshape(window_count, QWIN, HEADS, head_dim)
    keys_in = gathered[:, :, :channels].reshape(window_count, KWIN, HEADS, head_dim)
    values_in = gathered[:, :, channels:].reshape(window_count, KWIN, HEADS, head_dim)
    scores = jnp.einsum("wqhd,wkhd->whqk", query_blocks, keys_in, precision=PRECISE) / jnp.sqrt(
        float(head_dim)
    )
    query_codes = query_ids.reshape(window_count, QWIN)
    same_token = (query_codes[:, :, None] == key_ids[:, None, :]).astype(jnp.float32)
    scores = scores + token_bias[None, :, None, None] * same_token[:, None, :, :]
    usable_key = (key_ids > 0)[:, None, None, :]
    scores = jnp.where(usable_key, scores, -1e30)
    highest = lax.stop_gradient(jnp.max(scores, axis=-1, keepdims=True))
    weights = jnp.exp(scores - highest)
    weights = weights / jnp.sum(weights, axis=-1, keepdims=True)
    outcome = jnp.einsum("whqk,wkhd->wqhd", weights, values_in, precision=PRECISE)
    return outcome.reshape(window_count * QWIN, channels)


def place_rims(center, from_before, from_after):
    atoms_here = center.shape[1]
    lower = jnp.pad(from_before, ((0, 0), (0, atoms_here - HALO), (0, 0)))
    upper = jnp.pad(from_after, ((0, 0), (atoms_here - HALO, 0), (0, 0)))
    return center + lower + upper


def on_device(
    atom_state,
    atom_token,
    window_valid,
    attend_gain,
    project_weight,
    output_weight,
    token_bias,
    transit_gain,
    transit_weight,
    return_weight,
    cotangent,
):
    channels = atom_state.shape[2]
    atoms_here = atom_state.shape[1]
    query_ids = token_codes(atom_token, window_valid)
    ext_ids = with_halo(query_ids, (("atom", 0),), HALO)
    normed = normalize(atom_state, attend_gain).astype(jnp.bfloat16)
    query_part = project_weight[:, :channels]
    pair_part = project_weight[:, channels:]
    ext_normed = with_halo(normed, (("atom", 1),), HALO)
    queries = jnp.dot(normed, query_part, preferred_element_type=jnp.float32).astype(jnp.bfloat16)
    ext_pairs = jnp.dot(ext_normed, pair_part, preferred_element_type=jnp.float32).astype(
        jnp.bfloat16
    )

    def forward_one(operands):
        query_rows, pair_rows = operands
        return attend(
            query_rows.astype(jnp.float32),
            pair_rows.astype(jnp.float32),
            query_ids,
            ext_ids,
            token_bias,
        )

    attended = lax.map(forward_one, (queries, ext_pairs)).astype(jnp.bfloat16)
    residual = (
        atom_state.astype(jnp.float32)
        + jnp.dot(attended, output_weight, preferred_element_type=jnp.float32)
    ).astype(jnp.bfloat16)
    transit_in = normalize(residual, transit_gain).astype(jnp.bfloat16)
    both_parts = jnp.dot(transit_in, transit_weight, preferred_element_type=jnp.float32)
    gate_part = both_parts[:, :, :TRANS]
    up_part = both_parts[:, :, TRANS:]
    gated = (jax.nn.silu(gate_part) * up_part).astype(jnp.bfloat16)
    block_out = (
        residual.astype(jnp.float32)
        + jnp.dot(gated, return_weight, preferred_element_type=jnp.float32)
    ).astype(jnp.bfloat16)
    grad_return = jnp.einsum("sai,sac->ic", gated, cotangent, preferred_element_type=jnp.float32)
    back_gated = jnp.einsum(
        "sac,ic->sai", cotangent, return_weight, preferred_element_type=jnp.float32
    )
    sigmoid_gate = jax.nn.sigmoid(gate_part)
    back_gate = back_gated * up_part * sigmoid_gate * (1.0 + gate_part * (1.0 - sigmoid_gate))
    back_up = back_gated * gate_part * sigmoid_gate
    back_hidden = jnp.concatenate([back_gate, back_up], axis=-1).astype(jnp.bfloat16)
    grad_transit = jnp.einsum(
        "sac,sae->ce", transit_in, back_hidden, preferred_element_type=jnp.float32
    )
    back_transit = jnp.einsum(
        "sae,ce->sac", back_hidden, transit_weight, preferred_element_type=jnp.float32
    )
    _, pull_second = jax.vjp(normalize, residual.astype(jnp.float32), transit_gain)
    back_res_norm, grad_transit_gain = pull_second(back_transit)
    back_residual = cotangent.astype(jnp.float32) + back_res_norm
    back_res16 = back_residual.astype(jnp.bfloat16)
    grad_output = jnp.einsum(
        "sac,sae->ce", attended, back_res16, preferred_element_type=jnp.float32
    )
    back_attended = jnp.einsum(
        "sae,ce->sac", back_res16, output_weight, preferred_element_type=jnp.float32
    )

    def backward_one(operands):
        query_rows, pair_rows, back_rows = operands

        def local_attend(query_in, pairs_in, bias_in):
            return attend(query_in, pairs_in, query_ids, ext_ids, bias_in)

        _, pull_attend = jax.vjp(
            local_attend, query_rows.astype(jnp.float32), pair_rows.astype(jnp.float32), token_bias
        )
        return pull_attend(back_rows)

    back_queries, back_ext, bias_parts = lax.map(backward_one, (queries, ext_pairs, back_attended))
    grad_bias = jnp.sum(bias_parts, axis=0)
    grad_query = jnp.einsum(
        "sac,sae->ce", normed.astype(jnp.float32), back_queries, precision=PRECISE
    )
    grad_pairs = jnp.einsum(
        "sac,sae->ce", ext_normed.astype(jnp.float32), back_ext, precision=PRECISE
    )
    grad_project = jnp.concatenate([grad_query, grad_pairs], axis=1)
    back_ext_normed = jnp.einsum(
        "sae,ce->sac", back_ext, pair_part.astype(jnp.float32), precision=PRECISE
    )
    from_before = passed_along(
        back_ext_normed[:, HALO + atoms_here :].astype(jnp.bfloat16), "atom", 1
    ).astype(jnp.float32)
    from_after = passed_along(back_ext_normed[:, :HALO].astype(jnp.bfloat16), "atom", -1).astype(
        jnp.float32
    )
    own_rows = back_ext_normed[:, HALO : HALO + atoms_here] + jnp.einsum(
        "sae,ce->sac", back_queries, query_part.astype(jnp.float32), precision=PRECISE
    )
    back_normed = place_rims(own_rows, from_before, from_after)
    _, pull_first = jax.vjp(normalize, atom_state.astype(jnp.float32), attend_gain)
    back_state_norm, grad_attend_gain = pull_first(back_normed)
    state_grad = (back_residual + back_state_norm).astype(jnp.bfloat16)
    gradients = (
        grad_attend_gain,
        grad_project,
        grad_output,
        grad_bias,
        grad_transit_gain,
        grad_transit,
        grad_return,
    )
    totals = lax.psum(
        (
            gradients[0],
            gradients[1],
            gradients[2],
            gradients[3],
            gradients[4],
            gradients[5],
            gradients[6],
        ),
        ("samp", "atom"),
    )
    squares = sum((jnp.sum(member * member) for member in totals))
    factor = CLIP_NORM / jnp.sqrt(squares + CLIP_NORM * CLIP_NORM)
    clipped = tuple((member * factor for member in totals))
    return (
        block_out,
        state_grad,
        clipped[0],
        clipped[1],
        clipped[2],
        clipped[3],
        clipped[4],
        clipped[5],
        clipped[6],
    )


def solution(mesh):
    return jax.shard_map(
        on_device,
        mesh=mesh,
        in_specs=(
            P("samp", "atom", None),
            P("atom"),
            P("atom"),
            P(),
            P(),
            P(),
            P(),
            P(),
            P(),
            P(),
            P("samp", "atom", None),
        ),
        out_specs=(
            P("samp", "atom", None),
            P("samp", "atom", None),
            P(),
            P(),
            P(),
            P(),
            P(),
            P(),
            P(),
        ),
        check_vma=False,
    )
```

profile of v0, /device:TPU:0, one launch (start us, length us, event | category | flops | bytes accessed | tf_op | source)
XLA Modules:
  0.0 380.1 jit_solution(13928921964016010154)
XLA Ops:
  8.9 2.4 collective-permute-start.2
  16.6 5.1 %collective-permute-start = (bf16[4,48,128]{2,1,0:T(8,128)(2,1)S(1)}, bf16[4,48,128]{2,1,0:T(8,128)(2,1)S(1)}, u32[]{:S(2)}, u32[]{:S(2)}) collective-permute-start(bf16[4,48,128]{2,1,0:T(8,128)(2,1)S(1)} %get-tuple-element.304), channel_id=1, source_target_pairs={{0,1},{1,2},{2,3},{3,4},{4,5},{5,6},{6,7},{8,9},{9,10},{10,11},{11... | collective-permute-start | bytes 147464 | tf_op jit(solution)/shard_map/ppermute | solution.py:25
  27.4 67.5 %while.30 = (s32[]{:T(128)}, bf16[4,320,128]{2,1,0:T(8,128)(2,1)}, bf16[4,416,256]{2,1,0:T(8,128)(2,1)}, s32[10,1,1,128]{3,0,2,1:T(8,128)S(1)}, bf16[4,320,128]{...) while((s32[]{:T(128)}, bf16[4,320,128]{2,1,0:T(8,128)(2,1)}, ...), condition=%wide.region_5.6_spmd.clone, body=%wide.region_2.5_spmd.sunk.clone | while | flops 128473856 | bytes 16410097 | solution.py:127
  33.0 2.4 copy.101
  36.9 2.8 pad_maximum_fusion.13
  49.9 2.4 copy.101
  53.8 2.8 pad_maximum_fusion.13
  66.7 2.4 copy.101
  70.7 2.8 pad_maximum_fusion.13
  83.6 2.4 copy.101
  87.5 2.8 pad_maximum_fusion.13
  106.7 102.9 %while.31 = (s32[]{:T(128)}, f32[4,320,128]{2,1,0:T(8,128)}, f32[4,416,256]{2,1,0:T(8,128)}, f32[4,4]{1,0:T(4,128)S(1)}, s32[10,1,1,128]{3,0,2,1:T(8,128)S(1)}, ...) while((s32[]{:T(128)}, f32[4,320,128]{2,1,0:T(8,128)}, ...), condition=%wide.region_15.16_spmd.clone, body=%wide.region_10.15_spmd.sunk.clone | while | flops 319997184 | bytes 31044328 | solution.py:177
  114.3 2.4 copy.108
  116.7 2.4 copy.109
  119.2 2.8 pad_maximum_fusion.14
  139.9 2.4 copy.108
  142.4 2.4 copy.109
  144.8 2.8 pad_maximum_fusion.14
  165.6 2.4 copy.108
  168.1 2.4 copy.109
  170.5 2.8 pad_maximum_fusion.14
  191.3 2.4 copy.108
  193.7 2.4 copy.109
  196.2 2.8 pad_maximum_fusion.14
  209.6 2.5 fusion.84
  212.7 4.7 %collective-permute-start.4 = (bf16[4,48,128]{2,1,0:T(8,128)(2,1)S(1)}, bf16[4,48,128]{2,1,0:T(8,128)(2,1)S(1)}, u32[]{:S(2)}, u32[]{:S(2)}) collective-permute-start(bf16[4,48,128]{2,1,0:T(8,128)(2,1)S(1)} %get-tuple-element.302), channel_id=1, source_target_pairs={{0,1},{1,2},{2,3},{3,4},{4,5},{5,6},{6,7},{8,9},{9,10},{10,11},{11... | collective-permute-start | bytes 147464 | tf_op jit(solution)/shard_map/ppermute | solution.py:34
  221.2 1.8 fusion.42
  223.9 44.4 %all-reduce.8 = (f32[128]{0:T(128)S(1)}, f32[4]{0:T(128)S(1)}, f32[128]{0:T(128)S(1)}) all-reduce(f32[128]{0:T(128)S(1)} %get-tuple-element.226, f32[4]{0:T(128)S(1)} %reduce_sum.232, f32[128]{0:T(128)S(1)} %copy-done.29), channel_id=1, replica_groups=mesh['samp'=4,'atom'=8] {'samp','atom'}, use_global_device_ids=true, to_apply=%region_19.20 | all-reduce | flops 260 | bytes 2080 | tf_op jit(solution)/shard_map/psum | solution.py:211
  270.2 1.7 add_convert_fusion
  271.9 84.5 %all-reduce.12.cloned.1.call-done = (f32[128,384]{1,0:T(8,128)}, f32[128,128]{1,0:T(8,128)}, f32[128,512]{1,0:T(8,128)}, f32[256,128]{1,0:T(8,128)}) async-done(((f32[128,384]{1,0:T(8,128)}, f32[128,128]{1,0:T(8,128)}, f32[128,512]{1,0:T(8,128)}, f32[256,128]{1,0:T(8,128)}), (f32[128,384]{1,0:T(8,128)}, f32[128,128]{1,0:T(8,128)}, f32[128,512]{1,0:T(8,128)}, ...) | async-done | bytes 655376 | tf_op jit(solution)/shard_map/psum | solution.py:211
  358.0 1.6 multiply_reduce_fusion.5
  369.2 1.7 broadcast_multiply_fusion
  (341 shorter events, 158.1 us)
Async XLA Ops:
  7.2 89.7 %copy-start = (bf16[128,512]{1,0:T(8,128)(2,1)S(1)}, bf16[128,512]{1,0:T(8,128)(2,1)}, u32[]{:S(2)}) copy-start(bf16[128,512]{1,0:T(8,128)(2,1)} %param.23) | copy-start | bytes 393220
  7.2 16.6 %copy-start.15 = (bf16[128,384]{1,0:T(8,128)(2,1)S(1)}, bf16[128,384]{1,0:T(8,128)(2,1)}, u32[]{:S(2)}) copy-start(bf16[128,384]{1,0:T(8,128)(2,1)} %param.19) | copy-start | bytes 294916
  7.2 349.2 %all-reduce.12.cloned.1.call-start = ((), (), s32[]{:S(2)}) async-start(), calls=%async_computation | async-start | bytes 1310720 | tf_op jit(solution)/shard_map/psum | solution.py:211
  8.9 15.9 %collective-permute-start.2 = (s32[48]{0:T(128)S(1)}, s32[48]{0:T(128)S(1)}, u32[]{:S(2)}, u32[]{:S(2)}) collective-permute-start(s32[48]{0:T(128)S(1)} %get-tuple-element.310), channel_id=1, source_target_pairs={{0,1},{1,2},{2,3},{3,4},{4,5},{5,6},{6,7},{8,9},{9,10},{10,11},{11... | collective-permute-start | bytes 584 | tf_op jit(solution)/shard_map/ppermute | solution.py:25
  11.3 13.5 %collective-permute-start.3 = (s32[48]{0:T(128)S(1)}, s32[48]{0:T(128)S(1)}, u32[]{:S(2)}, u32[]{:S(2)}) collective-permute-start(s32[48]{0:T(128)S(1)} %get-tuple-element.311), channel_id=1, source_target_pairs={{1,0},{2,1},{3,2},{4,3},{5,4},{6,5},{7,6},{9,8},{10,9},{11,10},{12... | collective-permute-start | bytes 584 | tf_op jit(solution)/shard_map/ppermute | solution.py:26
  16.6 10.8 %copy-start.5 = (bf16[4,320,128]{2,1,0:T(8,128)(2,1)}, bf16[4,320,128]{2,1,0:T(8,128)(2,1)S(1)}, u32[]{:S(2)}) copy-start(bf16[4,320,128]{2,1,0:T(8,128)(2,1)S(1)} %fusion.39) | copy-start | bytes 983044
  16.6 9.1 %collective-permute-start = (bf16[4,48,128]{2,1,0:T(8,128)(2,1)S(1)}, bf16[4,48,128]{2,1,0:T(8,128)(2,1)S(1)}, u32[]{:S(2)}, u32[]{:S(2)}) collective-permute-start(bf16[4,48,128]{2,1,0:T(8,128)(2,1)S(1)} %get-tuple-element.304), channel_id=1, source_target_pairs={{0,1},{1,2},{2,3},{3,4},{4,5},{5,6},{6,7},{8,9},{9,10},{10,11},{11... | collective-permute-start | bytes 147464 | tf_op jit(solution)/shard_map/ppermute | solution.py:25
  21.7 4.4 %collective-permute-start.1 = (bf16[4,48,128]{2,1,0:T(8,128)(2,1)S(1)}, bf16[4,48,128]{2,1,0:T(8,128)(2,1)S(1)}, u32[]{:S(2)}, u32[]{:S(2)}) collective-permute-start(bf16[4,48,128]{2,1,0:T(8,128)(2,1)S(1)} %get-tuple-element.305), channel_id=1, source_target_pairs={{1,0},{2,1},{3,2},{4,3},{5,4},{6,5},{7,6},{9,8},{10,9},{11,10},{12... | collective-permute-start | bytes 147464 | tf_op jit(solution)/shard_map/ppermute | solution.py:26
  25.7 1.6 copy-start.20
  26.1 1.3 copy-start.22
  94.8 2.0 copy-start.25
  104.4 2.3 copy-start.7
  104.4 2.3 copy-start.19
  104.4 2.3 copy-start.26
  122.1 1.3 copy-start.1
  147.7 1.3 copy-start.1
  209.6 2.5 copy-start.27
  209.6 2.5 copy-start.6
  209.6 2.5 copy-start.12
  209.6 9.2 %copy-start.4 = (f32[4,416,256]{2,1,0:T(8,128)S(1)}, f32[4,416,256]{2,1,0:T(8,128)}, u32[]{:S(2)}) copy-start(f32[4,416,256]{2,1,0:T(8,128)} %get-tuple-element.221) | copy-start | bytes 5111812
  209.6 9.3 %copy-start.21 = (bf16[4,48,128]{2,1,0:T(8,128)(2,1)S(1)}, bf16[4,48,128]{2,1,0:T(8,128)(2,1)}, u32[]{:S(2)}) copy-start(bf16[4,48,128]{2,1,0:T(8,128)(2,1)} %copy-done.20) | copy-start | bytes 147460
  209.6 9.3 %copy-start.23 = (bf16[4,48,128]{2,1,0:T(8,128)(2,1)S(1)}, bf16[4,48,128]{2,1,0:T(8,128)(2,1)}, u32[]{:S(2)}) copy-start(bf16[4,48,128]{2,1,0:T(8,128)(2,1)} %copy-done.22) | copy-start | bytes 147460
  212.7 7.8 %collective-permute-start.4 = (bf16[4,48,128]{2,1,0:T(8,128)(2,1)S(1)}, bf16[4,48,128]{2,1,0:T(8,128)(2,1)S(1)}, u32[]{:S(2)}, u32[]{:S(2)}) collective-permute-start(bf16[4,48,128]{2,1,0:T(8,128)(2,1)S(1)} %get-tuple-element.302), channel_id=1, source_target_pairs={{0,1},{1,2},{2,3},{3,4},{4,5},{5,6},{6,7},{8,9},{9,10},{10,11},{11... | collective-permute-start | bytes 147464 | tf_op jit(solution)/shard_map/ppermute | solution.py:34
  217.4 3.1 copy-start.28
  217.4 3.8 copy-start.3
  217.4 3.8 copy-start.24
  217.4 3.7 collective-permute-start.5
  221.2 2.8 copy-start.29
  221.2 49.1 %copy-start.8 = (f32[4,320,128]{2,1,0:T(8,128)S(1)}, f32[4,320,128]{2,1,0:T(8,128)}, u32[]{:S(2)}) copy-start(f32[4,320,128]{2,1,0:T(8,128)} %copy-done.7) | copy-start | bytes 1966084
  221.2 49.1 %copy-start.10 = (bf16[4,320,128]{2,1,0:T(8,128)(2,1)S(1)}, bf16[4,320,128]{2,1,0:T(8,128)(2,1)}, u32[]{:S(2)}) copy-start(bf16[4,320,128]{2,1,0:T(8,128)(2,1)} %param.25) | copy-start | bytes 983044
  356.4 15.1 %copy-start.14 = (f32[128,128]{1,0:T(8,128)S(1)}, f32[128,128]{1,0:T(8,128)}, u32[]{:S(2)}) copy-start(f32[128,128]{1,0:T(8,128)} %get-tuple-element.270) | copy-start | bytes 196612
  356.4 15.7 %copy-start.13 = (f32[128,384]{1,0:T(8,128)S(1)}, f32[128,384]{1,0:T(8,128)}, u32[]{:S(2)}) copy-start(f32[128,384]{1,0:T(8,128)} %get-tuple-element.269) | copy-start | bytes 589828
  (14 other events, 14.2 us)
Sparse Core Ops, SparseCore 0:
  220.6 135.7 all-reduce.11
where the time goes:
time: 383 us; the launch traced here: 380 us
  local copies, waits for them, and re-layouts  96.1 us (25%)
  waiting for transfers between devices  85.5 us (22%)
  other arithmetic  71.7 us (19%)
  matrix products  46 us (12%)
  blocking collectives  44.4 us (12%)
  between operations  19 us (5%)
  starting transfers between devices  16.2 us (4%)
    psum x1, waiting for transfers between devices, on_device(): lax.psum((gradients[0], gradients[1], gradients[2], gradients[3], gradien...  84.5 us
    slice x40, local copies, waits for them, and re-layouts, attend(): blocks[offset:offset + window_count]  57.2 us
    psum x1, blocking collectives, on_device(): lax.psum((gradients[0], gradients[1], gradients[2], gradients[3], gradien...  44.4 us
    concatenate x8, other arithmetic, attend(): jnp.concatenate([blocks[offset:offset + window_count] for offset in range...  22.3 us
    dot_general x12, matrix products, attend(): jnp.einsum('whqk,wkhd->wqhd', weights, values_in, precision=PRECISE)  16.2 us
    dot_general x16, matrix products, attend(): jnp.einsum('wqhd,wkhd->whqk', query_blocks, keys_in, precision=PRECISE)  12.1 us
    reduce_sum x7, other arithmetic, on_device(): squares = sum((jnp.sum(member * member) for member in totals))  8.12 us
  transfers between devices with their start and end apart: 7, of which 3 were waited for; matrix products, arithmetic and copies ran while one was open for 4% of the time, Pallas kernels for 0%

commit v1 on v0

v1 whole, which is shorter than its diff:
```python
import functools

import jax
import jax.numpy as jnp
from jax import lax
from jax.experimental import pallas as pl
from jax.experimental.pallas import tpu as pltpu
from jax.sharding import PartitionSpec as P

HEADS = 4
TRANS = 256
QWIN = 32
KWIN = 128
HALO = 48
EPSILON = 1e-05
CLIP_NORM = 256.0
BF = jnp.bfloat16
F32 = jnp.float32
LANES = 128
MESH = pl.DeviceIdType.MESH


def dot(a, b, dims=((1,), (0,))):
    return lax.dot_general(a, b, (dims, ((), ())), preferred_element_type=F32)


def dot_nt(a, b):
    return dot(a, b, ((1,), (1,)))


def dot_tn(a, b):
    return dot(a, b, ((0,), (0,)))


def stats(x):
    center = jnp.mean(x, axis=-1, keepdims=True)
    shifted = x - center
    rstd = lax.rsqrt(jnp.mean(shifted * shifted, axis=-1, keepdims=True) + EPSILON)
    return shifted * rstd, rstd


def norm_back(back, xhat, rstd, gain):
    scaled = back * gain
    first = jnp.mean(scaled, axis=-1, keepdims=True)
    second = jnp.mean(scaled * xhat, axis=-1, keepdims=True)
    return rstd * (scaled - first - xhat * second)


def split_hi_lo(row):
    hi = row.astype(BF)
    return hi, (row - hi.astype(F32)).astype(BF)


def local_kernel(
    ext_ref, cot_ref, kid_ref, qid_ref, again_ref, wp_ref, wo_ref, bias_ref, tgain_ref, wt_ref, wr_ref,
    out_ref, bnorm_ref, bres_ref, halo_ref, g_ref,
    normed_ref, q_ref, kv_ref, p_ref, att_ref, batt_ref, bq_ref, bkv_ref, mask_ref, same_ref, acc_ref, row_ref,
):
    samples, atoms, width = cot_ref.shape
    windows = atoms // QWIN
    hd = width // HEADS
    scale = 1.0 / (float(hd) ** 0.5)
    rows_h = lax.broadcasted_iota(jnp.int32, (HEADS * QWIN, width), 0) // QWIN
    cols_h = lax.broadcasted_iota(jnp.int32, (HEADS * QWIN, width), 1) // hd
    head_f = (rows_h == cols_h).astype(F32)
    head_b = head_f.astype(BF)
    again = again_ref[...]
    tgain = tgain_ref[...]

    acc_ref[...] = jnp.zeros_like(acc_ref)
    row_ref[...] = jnp.zeros_like(row_ref)
    bkv_ref[...] = jnp.zeros_like(bkv_ref)

    def masks(w, _):
        base = pl.multiple_of(w * QWIN, QWIN)
        kid = kid_ref[pl.ds(base, KWIN), :]
        same = (kid == qid_ref[pl.ds(w, 1), :]).astype(F32)
        same_ref[w] = same
        mask_ref[w] = jnp.where(kid > 0, same * bias_ref[...], -1e30)
        return 0

    lax.fori_loop(0, windows, masks, 0)

    def project(s, _):
        xhat, _r = stats(ext_ref[s].astype(F32))
        normed = (xhat * again).astype(BF)
        normed_ref[s] = normed
        both = dot(normed, wp_ref[...]).astype(BF)
        q_ref[s] = both[HALO : HALO + atoms, :width]
        kv_ref[s] = both[:, width:]
        return 0

    lax.fori_loop(0, samples, project, 0)

    def spread(rows):
        return jnp.concatenate([rows] * HEADS, axis=0) * head_b

    def gather_heads(value):
        return jnp.sum((value * head_f).reshape(HEADS, QWIN, width), axis=0)

    def attend(w, _):
        base = pl.multiple_of(w * QWIN, QWIN)
        mask = mask_ref[w]
        for s in range(samples):
            keys = kv_ref[s, pl.ds(base, KWIN), :width]
            vals = kv_ref[s, pl.ds(base, KWIN), width:]
            score = dot_nt(keys, spread(q_ref[s, pl.ds(base, QWIN), :])) * scale + mask
            weight = jnp.exp(score - jnp.max(score, axis=0, keepdims=True))
            prob = (weight * (1.0 / jnp.sum(weight, axis=0, keepdims=True))).astype(BF)
            p_ref[s, w] = prob
            att_ref[s, pl.ds(base, QWIN), :] = gather_heads(dot_tn(prob, vals)).astype(BF)
        return 0

    lax.fori_loop(0, windows, attend, 0)

    def transit(s, _):
        state = ext_ref[s, HALO : HALO + atoms, :].astype(F32)
        att = att_ref[s]
        residual = (state + dot(att, wo_ref[...])).astype(BF).astype(F32)
        xhat, rstd = stats(residual)
        tin = (xhat * tgain).astype(BF)
        both = dot(tin, wt_ref[...])
        gate, up = both[:, :TRANS], both[:, TRANS:]
        sig = 1.0 / (1.0 + jnp.exp(-gate))
        silu = gate * sig
        gated = (silu * up).astype(BF)
        out_ref[s] = (residual + dot(gated, wr_ref[...])).astype(BF)
        cot = cot_ref[s]
        acc_ref[8:10] += dot_tn(gated, cot).reshape(2, LANES, LANES)
        bg = dot_nt(cot, wr_ref[...])
        back_gate = (bg * up * sig * (1.0 + gate * (1.0 - sig))).astype(BF)
        back_up = (bg * silu).astype(BF)
        bh = jnp.concatenate([back_gate, back_up], axis=1)
        gt = dot_tn(tin, bh)
        for j in range(4):
            acc_ref[4 + j] += gt[:, j * LANES : (j + 1) * LANES]
        bt = dot_nt(bh, wt_ref[...])
        row_ref[1:2] += jnp.sum(bt * xhat, axis=0, keepdims=True)
        bres = cot.astype(F32) + norm_back(bt, xhat, rstd, tgain)
        bres_ref[s] = bres
        b16 = bres.astype(BF)
        acc_ref[3] += dot_tn(att, b16)
        batt_ref[s] = dot_nt(b16, wo_ref[...]).astype(BF)
        return 0

    lax.fori_loop(0, samples, transit, 0)

    def attend_back(w, _):
        base = pl.multiple_of(w * QWIN, QWIN)
        total = jnp.zeros((KWIN, LANES), F32)
        for s in range(samples):
            keys = kv_ref[s, pl.ds(base, KWIN), :width]
            vals = kv_ref[s, pl.ds(base, KWIN), width:]
            qs = spread(q_ref[s, pl.ds(base, QWIN), :])
            bo = spread(batt_ref[s, pl.ds(base, QWIN), :])
            prob = p_ref[s, w]
            pf = prob.astype(F32)
            bp = dot_nt(vals, bo)
            pbp = pf * bp
            bs = pbp - pf * jnp.sum(pbp, axis=0, keepdims=True)
            total = total + bs
            b16 = (bs * scale).astype(BF)
            bq_ref[s, pl.ds(base, QWIN), :] = gather_heads(dot_tn(b16, keys)).astype(BF)
            bkv_ref[s, pl.ds(base, KWIN), :width] += dot(b16, qs)
            bkv_ref[s, pl.ds(base, KWIN), width:] += dot(prob, bo)
        row_ref[2:3] += jnp.sum(total * same_ref[w], axis=0, keepdims=True)
        return 0

    lax.fori_loop(0, windows, attend_back, 0)

    def finish(s, _):
        normed = normed_ref[s]
        bkv = bkv_ref[s].astype(BF)
        bq = bq_ref[s]
        acc_ref[0] += dot_tn(normed[HALO : HALO + atoms], bq)
        gkv = dot_tn(normed, bkv)
        acc_ref[1] += gkv[:, :LANES]
        acc_ref[2] += gkv[:, LANES:]
        back = dot_nt(bkv, wp_ref[:, width:])
        own = back[HALO : HALO + atoms] + dot_nt(bq, wp_ref[:, :width])
        xhat, _r = stats(ext_ref[s].astype(F32))
        halo_before = back[:HALO]
        halo_after = back[HALO + atoms :]
        row_ref[0:1] += (
            jnp.sum(own * xhat[HALO : HALO + atoms], axis=0, keepdims=True)
            + jnp.sum(halo_before * xhat[:HALO], axis=0, keepdims=True)
            + jnp.sum(halo_after * xhat[HALO + atoms :], axis=0, keepdims=True)
        )
        halo_ref[0, s] = halo_after.astype(BF)
        halo_ref[1, s] = halo_before.astype(BF)
        bnorm_ref[s] = own
        return 0

    lax.fori_loop(0, samples, finish, 0)

    blocks = acc_ref.shape[0]
    g_ref[: blocks * LANES, :] = acc_ref[...].reshape(blocks * LANES, LANES).astype(BF)
    rest = g_ref.shape[0] - blocks * LANES
    pieces = []
    for i in range(3):
        hi, lo = split_hi_lo(row_ref[i : i + 1])
        pieces += [hi.astype(F32), lo.astype(F32)]
    pieces.append(jnp.zeros((rest - 6, LANES), F32))
    g_ref[blocks * LANES :, :] = jnp.concatenate(pieces, axis=0).astype(BF)


def reduce_kernel(
    A, S,
    g_ref, halo_ref, bnorm_ref, bres_ref, state_ref, again_ref,
    sg_ref, gag_ref, gp_ref, go_ref, gb_ref, gtg_ref, gt_ref, gr_ref,
    recv1, send2, recv2, gath, rim,
    s1, r1, s2, r2, s3, r3, s4, r4, sh, rh,
):
    me_s, me_a = lax.axis_index("samp"), lax.axis_index("atom")
    samples, atoms, width = state_ref.shape

    barrier = pltpu.get_barrier_semaphore()
    for d in range(1, A):
        pl.semaphore_signal(barrier, inc=1, device_id=(me_s, lax.rem(me_a + d, A)), device_id_type=MESH)
    for d in range(1, S):
        pl.semaphore_signal(barrier, inc=1, device_id=(lax.rem(me_s + d, S), me_a), device_id_type=MESH)
    pl.semaphore_wait(barrier, A + S - 2)

    def remote(src, dst, ss, rs, dev):
        return pltpu.make_async_remote_copy(
            src_ref=src, dst_ref=dst, send_sem=ss, recv_sem=rs, device_id=dev, device_id_type=MESH
        )

    first = []
    for d in range(1, A):
        peer = lax.rem(me_a + d, A)
        copy = remote(g_ref.at[peer], recv1.at[d - 1], s1.at[d - 1], r1.at[d - 1], (me_s, peer))
        copy.start()
        first.append(copy)

    up = remote(halo_ref.at[0], rim.at[0], sh.at[0], rh.at[0], (me_s, lax.rem(me_a + 1, A)))
    down = remote(halo_ref.at[1], rim.at[1], sh.at[1], rh.at[1], (me_s, lax.rem(me_a + A - 1, A)))
    up.start()
    down.start()

    total = g_ref[me_a].astype(F32)
    for d in range(1, A):
        first[d - 1].wait_recv()
        total = total + recv1[d - 1].astype(F32)
    send2[...] = total.astype(BF)

    second = []
    for d in range(1, S):
        peer = lax.rem(me_s + d, S)
        copy = remote(send2.at[peer], recv2.at[d - 1], s2.at[d - 1], r2.at[d - 1], (peer, me_a))
        copy.start()
        second.append(copy)

    up.wait()
    down.wait()
    has_before = (me_a > 0).astype(F32)
    has_after = (me_a < A - 1).astype(F32)
    again = again_ref[...]

    def one(s, _):
        xhat, rstd = stats(state_ref[s].astype(F32))
        own = bnorm_ref[s]
        head = own[:HALO] + rim[0, s].astype(F32) * has_before
        tail = own[atoms - HALO :] + rim[1, s].astype(F32) * has_after
        back = jnp.concatenate([head, own[HALO : atoms - HALO], tail], axis=0)
        sg_ref[s] = (bres_ref[s] + norm_back(back, xhat, rstd, again)).astype(BF)
        return 0

    mine = send2[me_s].astype(F32)
    for d in range(1, S):
        second[d - 1].wait_recv()
        mine = mine + recv2[d - 1].astype(F32)
    gath[me_a, me_s] = mine.astype(BF)

    third = []
    for d in range(1, S):
        peer = lax.rem(me_s + d, S)
        copy = remote(gath.at[me_a, me_s], gath.at[me_a, me_s], s3.at[d - 1], r3.at[d - 1], (peer, me_a))
        copy.start()
        third.append(copy)
    for d in range(1, S):
        src = lax.rem(me_s + S - d, S)
        remote(gath.at[me_a, src], gath.at[me_a, src], s3.at[d - 1], r3.at[d - 1], (src, me_a)).wait_recv()
    fourth = []
    for d in range(1, A):
        peer = lax.rem(me_a + d, A)
        copy = remote(gath.at[me_a], gath.at[me_a], s4.at[d - 1], r4.at[d - 1], (me_s, peer))
        copy.start()
        fourth.append(copy)

    lax.fori_loop(0, samples, one, 0)

    for d in range(1, A):
        src = lax.rem(me_a + A - d, A)
        remote(gath.at[src], gath.at[src], s4.at[d - 1], r4.at[d - 1], (me_s, src)).wait_recv()
    for copy in first + second + third + fourth:
        copy.wait_send()

    flat = gath[...].astype(F32).reshape(-1, LANES)
    blocks = [flat[j * LANES : (j + 1) * LANES] for j in range(10)]
    rest = flat[10 * LANES : 10 * LANES + 6]
    rows = [rest[0:1] + rest[1:2], rest[2:3] + rest[3:4], rest[4:5] + rest[5:6]]
    lane_head = lax.broadcasted_iota(jnp.int32, (1, LANES), 1)
    bias = jnp.zeros((1, LANES), F32)
    for h in range(HEADS):
        part = jnp.sum(jnp.where(lane_head // QWIN == h, rows[2], 0.0), axis=1, keepdims=True)
        bias = bias + jnp.where(lane_head == h, part, 0.0)
    sq = blocks[0] * blocks[0]
    for b in blocks[1:]:
        sq = sq + b * b
    sq = jnp.sum(sq, axis=0, keepdims=True) + rows[0] * rows[0] + rows[1] * rows[1] + bias * bias
    squares = jnp.sum(sq, axis=1, keepdims=True)
    factor = CLIP_NORM / jnp.sqrt(squares + CLIP_NORM * CLIP_NORM)
    gag_ref[...] = rows[0] * factor
    gtg_ref[...] = rows[1] * factor
    gb_ref[...] = bias * factor
    for j in range(3):
        gp_ref[:, j * LANES : (j + 1) * LANES] = blocks[j] * factor
    go_ref[...] = blocks[3] * factor
    for j in range(4):
        gt_ref[:, j * LANES : (j + 1) * LANES] = blocks[4 + j] * factor
    for j in range(2):
        gr_ref[j * LANES : (j + 1) * LANES, :] = blocks[8 + j] * factor


def on_device(A, S, atom_state, atom_token, window_valid, attend_gain, project_weight, output_weight,
              token_bias, transit_gain, transit_weight, return_weight, cotangent):
    samples, atoms, width = atom_state.shape
    windows = window_valid.shape[0]
    ext = atoms + 2 * HALO
    up_pairs = [(i, i + 1) for i in range(A - 1)]
    down_pairs = [(i + 1, i) for i in range(A - 1)]
    slots = lax.broadcasted_iota(jnp.int32, (windows, QWIN), 1)
    ids = jnp.where((slots < window_valid[:, None]).reshape(-1), atom_token + 1, 0)
    before = lax.ppermute(atom_state[:, atoms - HALO :], "atom", up_pairs)
    after = lax.ppermute(atom_state[:, :HALO], "atom", down_pairs)
    ids_before = lax.ppermute(ids[atoms - HALO :], "atom", up_pairs)
    ids_after = lax.ppermute(ids[:HALO], "atom", down_pairs)
    ext_state = jnp.concatenate([before, atom_state, after], axis=1)
    ext_ids = jnp.concatenate([ids_before, ids, ids_after])
    kid = jnp.broadcast_to(ext_ids[:, None], (ext, LANES))
    qid = jnp.tile(ids.reshape(windows, QWIN), (1, HEADS))
    again = attend_gain.reshape(1, width)
    tgain = transit_gain.reshape(1, width)
    bias_row = jnp.repeat(token_bias, QWIN).reshape(1, HEADS * QWIN)
    shards = A * S
    need = 10 * LANES + 6
    per = -(-need // (shards * 16)) * 16
    vm = pl.BlockSpec(memory_space=pltpu.VMEM)
    sds = jax.ShapeDtypeStruct
    act = (samples, atoms, width)
    block_out, bnorm, bres, halo, grads = pl.pallas_call(
        local_kernel,
        out_shape=(sds(act, BF), sds(act, F32), sds(act, F32), sds((2, samples, HALO, width), BF),
                   sds((shards * per, LANES), BF)),
        in_specs=[vm] * 11,
        out_specs=(vm,) * 5,
        scratch_shapes=[
            pltpu.VMEM((samples, ext, width), BF),
            pltpu.VMEM(act, BF),
            pltpu.VMEM((samples, ext, 2 * width), BF),
            pltpu.VMEM((samples, windows, KWIN, LANES), BF),
            pltpu.VMEM(act, BF),
            pltpu.VMEM(act, BF),
            pltpu.VMEM(act, BF),
            pltpu.VMEM((samples, ext, 2 * width), F32),
            pltpu.VMEM((windows, KWIN, LANES), F32),
            pltpu.VMEM((windows, KWIN, LANES), F32),
            pltpu.VMEM((10, LANES, LANES), F32),
            pltpu.VMEM((8, LANES), F32),
        ],
        name="local",
    )(ext_state, cotangent, kid, qid, again, project_weight, output_weight, bias_row, tgain,
      transit_weight, return_weight)
    grads = grads.reshape(A, S, per, LANES)
    dma = pltpu.SemaphoreType.DMA
    sg, gag, gp, go, gb, gtg, gt, gr = pl.pallas_call(
        functools.partial(reduce_kernel, A, S),
        out_shape=(sds(act, BF), sds((1, width), F32), sds((width, 3 * width), F32), sds((width, width), F32),
                   sds((1, LANES), F32), sds((1, width), F32), sds((width, 2 * TRANS), F32),
                   sds((TRANS, width), F32)),
        in_specs=[vm] * 6,
        out_specs=(vm,) * 8,
        scratch_shapes=[
            pltpu.VMEM((A - 1, S, per, LANES), BF),
            pltpu.VMEM((S, per, LANES), BF),
            pltpu.VMEM((S - 1, per, LANES), BF),
            pltpu.VMEM((A, S, per, LANES), BF),
            pltpu.VMEM((2, samples, HALO, width), BF),
            dma((A - 1,)), dma((A - 1,)), dma((S - 1,)), dma((S - 1,)), dma((S - 1,)), dma((S - 1,)),
            dma((A - 1,)), dma((A - 1,)), dma((2,)), dma((2,)),
        ],
        compiler_params=pltpu.CompilerParams(collective_id=0, has_side_effects=True),
        name="reduce",
    )(grads, halo, bnorm, bres, atom_state, again)
    return (block_out, sg, gag.reshape(width), gp, go, gb[0, :HEADS], gtg.reshape(width), gt, gr)


def solution(mesh):
    A, S = mesh.shape["atom"], mesh.shape["samp"]
    act = P("samp", "atom", None)
    return jax.shard_map(
        functools.partial(on_device, A, S),
        mesh=mesh,
        in_specs=(act, P("atom"), P("atom"), P(), P(), P(), P(), P(), P(), P(), act),
        out_specs=(act, act, P(), P(), P(), P(), P(), P(), P()),
        check_vma=False,
    )
```

time: 383 us -> 89.4 us (0.23)
  local copies, waits for them, and re-layouts: 96.1 us -> 10.3 us
  waiting for transfers between devices: 85.5 us -> 1.55 us
  other arithmetic: 71.7 us -> 2.59 us
  Pallas kernels: 0 us -> 63.7 us
  matrix products: 46 us -> 0 us
  blocking collectives: 44.4 us -> 0 us
  between operations: 19 us -> 0.73 us
  starting transfers between devices: 16.2 us -> 10.1 us
    psum x1 -> x0, waiting for transfers between devices: 84.5 us -> none  [on_device(): lax.psum((gradients[0], gradients[1], gradients[2], gradients[3], gradien...]
    pallas_call x0 -> x2, Pallas kernels: none -> 63.7 us  [the longest x1 35.5 us: on_device(): pl.pallas_call(local_kernel, out_shape=(sds(act, BF), sds(act, F32), sds(...]
    slice x56 -> x2, local copies, waits for them, and re-layouts: 58.5 us -> 0.91 us  [the longest x1 0.84 us: on_device(): before = lax.ppermute(atom_state[:, atoms - HALO:], 'atom', up_pairs)]
    dot_general x43 -> x0, matrix products: 46 us -> none  [the longest x12 16.2 us: attend(): jnp.einsum('whqk,wkhd->wqhd', weights, values_in, precision=PRECISE)]
    psum x1 -> x0, blocking collectives: 44.4 us -> none  [on_device(): lax.psum((gradients[0], gradients[1], gradients[2], gradients[3], gradien...]
    concatenate x12 -> x2, other arithmetic: 23.2 us -> 1.85 us  [the longest x1 1.77 us: on_device(): ext_state = jnp.concatenate([before, atom_state, after], axis=1)]
    reduce_sum x25 -> x0, other arithmetic: 19.6 us -> none  [the longest x7 8.12 us: on_device(): squares = sum((jnp.sum(member * member) for member in totals))]
    convert_element_type x19 -> x0, other arithmetic: 14.6 us -> none  [the longest x4 3.87 us: forward_one(): pair_rows.astype(jnp.float32)]
  transfers between devices with their start and end apart: 7 -> 4, of which waited for: 3 -> 1; matrix products, arithmetic and copies ran while one was open for 4% -> 3% of each run, Pallas kernels for 0% -> 0%
where the time goes in v1:
time: 89.4 us; the launch traced here: 88.9 us
  Pallas kernels  63.7 us (71%)
  local copies, waits for them, and re-layouts  10.3 us (12%)
  starting transfers between devices  10.1 us (11%)
  other arithmetic  2.59 us (3%)
  waiting for transfers between devices  1.55 us (2%)
    pallas_call x1, Pallas kernels, on_device(): pl.pallas_call(local_kernel, out_shape=(sds(act, BF), sds(act, F32), sds(...  35.5 us
    pallas_call x1, Pallas kernels, on_device(): pl.pallas_call(functools.partial(reduce_kernel, A, S), out_shape=(sds(act...  28.2 us
    unnamed x25, local copies, waits for them, and re-layouts  6.58 us
    ppermute x1, starting transfers between devices, on_device(): before = lax.ppermute(atom_state[:, atoms - HALO:], 'atom', up_pairs)  5.12 us
    ppermute x1, starting transfers between devices, on_device(): ids_before = lax.ppermute(ids[atoms - HALO:], 'atom', up_pairs)  2.39 us
  transfers between devices with their start and end apart: 4, of which 1 were waited for; matrix products, arithmetic and copies ran while one was open for 3% of the time, Pallas kernels for 0%

profile of v1, /device:TPU:0, one launch (start us, length us, event | category | flops | bytes accessed | tf_op | source)
XLA Modules:
  0.0 88.9 jit_solution(10419625091775184587)
XLA Ops:
  0.7 0.7 iota_compare_fusion
  1.4 0.1 lt.14
  1.5 0.1 fusion.1
  1.6 2.4 %collective-permute-start.2 = (s32[48]{0:T(128)S(1)}, s32[48]{0:T(128)S(1)}, u32[]{:S(2)}, u32[]{:S(2)}) collective-permute-start(s32[48]{0:T(128)S(1)} %get-tuple-element.37), channel_id=1, source_target_pairs={{0,1},{1,2},{2,3},{3,4},{4,5},{5,6},{6,7},{8,9},{9,10},{10,11},{11... | collective-permute-start | bytes 584 | tf_op jit(solution)/shard_map/ppermute | solution.py:337
  4.0 1.3 %collective-permute-start.3 = (s32[48]{0:T(128)S(1)}, s32[48]{0:T(128)S(1)}, u32[]{:S(2)}, u32[]{:S(2)}) collective-permute-start(s32[48]{0:T(128)S(1)} %get-tuple-element.38), channel_id=1, source_target_pairs={{1,0},{2,1},{3,2},{4,3},{5,4},{6,5},{7,6},{9,8},{10,9},{11,10},{12... | collective-permute-start | bytes 584 | tf_op jit(solution)/shard_map/ppermute | solution.py:338
  5.3 0.8 fusion
  6.1 5.1 %collective-permute-start = (bf16[4,48,128]{2,1,0:T(8,128)(2,1)S(1)}, bf16[4,48,128]{2,1,0:T(8,128)(2,1)S(1)}, u32[]{:S(2)}, u32[]{:S(2)}) collective-permute-start(bf16[4,48,128]{2,1,0:T(8,128)(2,1)S(1)} %get-tuple-element.35), channel_id=1, source_target_pairs={{0,1},{1,2},{2,3},{3,4},{4,5},{5,6},{6,7},{8,9},{9,10},{10,11},{11... | collective-permute-start | bytes 147464 | tf_op jit(solution)/shard_map/ppermute | solution.py:335
  11.2 0.0 copy-start.5
  11.2 1.3 %collective-permute-start.1 = (bf16[4,48,128]{2,1,0:T(8,128)(2,1)S(1)}, bf16[4,48,128]{2,1,0:T(8,128)(2,1)S(1)}, u32[]{:S(2)}, u32[]{:S(2)}) collective-permute-start(bf16[4,48,128]{2,1,0:T(8,128)(2,1)S(1)} %get-tuple-element.36), channel_id=1, source_target_pairs={{1,0},{2,1},{3,2},{4,3},{5,4},{6,5},{7,6},{9,8},{10,9},{11,10},{12... | collective-permute-start | bytes 147464 | tf_op jit(solution)/shard_map/ppermute | solution.py:336
  12.5 0.1 tile.10
  12.6 0.1 broadcast_in_dim.16
  12.7 0.6 reshape_reshape.3.bias_ref
  13.3 0.7 tile.12.qid_ref
  14.0 0.0 collective-permute-done.2
  14.0 0.1 pad_add_fusion
  14.0 0.0 collective-permute-done
  14.0 1.5 %collective-permute-done.1 = bf16[4,48,128]{2,1,0:T(8,128)(2,1)S(1)} collective-permute-done((bf16[4,48,128]{2,1,0:T(8,128)(2,1)S(1)}, bf16[4,48,128]{2,1,0:T(8,128)(2,1)S(1)}, u32[]{:S(2)}, u32[]{:S(2)}) %collective-permute-start.1) | collective-permute-done | bytes 49184 | tf_op jit(solution)/shard_map/ppermute | solution.py:336
  15.6 1.8 %pad_maximum_fusion.ext_ref = bf16[4,416,128]{2,1,0:T(8,128)(2,1)} fusion(bf16[4,48,128]{2,1,0:T(8,128)(2,1)S(1)} %collective-permute-done.1, bf16[4,320,128]{2,1,0:T(8,128)(2,1)} %state_ref.1, bf16[4,48,128]{2,1,0:T(8,128)(2,1)S(1)} %collective-permute-done), kind=kLoop, calls=%fused_computation | loop fusion | flops 1277952 | bytes 851968 | tf_op jit(solution)/shard_map/concatenate | solution.py:339
  17.4 0.8 broadcast_in_dim.15.kid_ref
  18.2 35.5 %local.1 = (bf16[4,320,128]{2,1,0:T(8,128)(2,1)}, f32[4,320,128]{2,1,0:T(8,128)}, f32[4,320,128]{2,1,0:T(8,128)}, bf16[2,4,48,128]{3,2,1,0:T(8,128)(2,1)}, bf16[1536,128]{1,0:T(8,128)(2,1)}) custom-call(bf16[4,416,128]{2,1,0:T(8,128)(2,1)} %pad_maximum_fusion.ext_ref, bf16[4,320,128]{2,1,0:T(8,128)(2,1)} %cot_ref.1, s32[416,128]{1,0:T(8,128)} %broadcast_in_dim.15.kid_ref, ...), custom_call_target="tpu_custom_call" | custom-call | tf_op jit(solution)/shard_map/local/pallas_call | solution.py:352
  53.6 28.2 %reduce.1 = (bf16[4,320,128]{2,1,0:T(8,128)(2,1)}, f32[1,128]{1,0:T(1,128)}, f32[128,384]{1,0:T(8,128)}, f32[128,128]{1,0:T(8,128)}, f32[1,128]{1,0:T(1,128)}, /...) custom-call(bf16[8,4,48,128]{3,2,1,0:T(8,128)(2,1)} %bitcast.7, ...), custom_call_target="tpu_custom_call" | custom-call | tf_op jit(solution)/shard_map/reduce/pallas_call | solution.py:377
  81.9 0.6 copy-done.8
  82.5 0.5 slice_bitcast_fusion
  83.0 1.8 %copy.27 = bf16[4,320,128]{2,1,0:T(8,128)(2,1)} copy(bf16[4,320,128]{2,1,0:T(8,128)(2,1)} %get-tuple-element.49) | data formatting | bytes 655360
  84.8 0.5 copy.28
  85.3 0.7 copy.29
  86.0 0.2 copy-done.3
  86.1 0.6 copy.30
  86.8 0.5 copy.31
  87.3 0.7 copy.32
  88.0 0.3 copy-done.2
  88.3 0.7 copy.33
  (17 shorter events, 0.0 us)
Async XLA Ops:
  0.6 0.8 copy-start.4
  1.6 12.4 %collective-permute-start.2 = (s32[48]{0:T(128)S(1)}, s32[48]{0:T(128)S(1)}, u32[]{:S(2)}, u32[]{:S(2)}) collective-permute-start(s32[48]{0:T(128)S(1)} %get-tuple-element.37), channel_id=1, source_target_pairs={{0,1},{1,2},{2,3},{3,4},{4,5},{5,6},{6,7},{8,9},{9,10},{10,11},{11... | collective-permute-start | bytes 584 | tf_op jit(solution)/shard_map/ppermute | solution.py:337
  4.0 10.0 %collective-permute-start.3 = (s32[48]{0:T(128)S(1)}, s32[48]{0:T(128)S(1)}, u32[]{:S(2)}, u32[]{:S(2)}) collective-permute-start(s32[48]{0:T(128)S(1)} %get-tuple-element.38), channel_id=1, source_target_pairs={{1,0},{2,1},{3,2},{4,3},{5,4},{6,5},{7,6},{9,8},{10,9},{11,10},{12... | collective-permute-start | bytes 584 | tf_op jit(solution)/shard_map/ppermute | solution.py:338
  6.1 8.0 %collective-permute-start = (bf16[4,48,128]{2,1,0:T(8,128)(2,1)S(1)}, bf16[4,48,128]{2,1,0:T(8,128)(2,1)S(1)}, u32[]{:S(2)}, u32[]{:S(2)}) collective-permute-start(bf16[4,48,128]{2,1,0:T(8,128)(2,1)S(1)} %get-tuple-element.35), channel_id=1, source_target_pairs={{0,1},{1,2},{2,3},{3,4},{4,5},{5,6},{6,7},{8,9},{9,10},{10,11},{11... | collective-permute-start | bytes 147464 | tf_op jit(solution)/shard_map/ppermute | solution.py:335
  11.2 1.4 %copy-start.5 = (f32[4]{0:T(128)S(1)}, f32[4]{0:T(128)}, u32[]{:S(2)}) copy-start(f32[4]{0:T(128)} %param.17) | copy-start | bytes 52
  11.2 4.4 %collective-permute-start.1 = (bf16[4,48,128]{2,1,0:T(8,128)(2,1)S(1)}, bf16[4,48,128]{2,1,0:T(8,128)(2,1)S(1)}, u32[]{:S(2)}, u32[]{:S(2)}) collective-permute-start(bf16[4,48,128]{2,1,0:T(8,128)(2,1)S(1)} %get-tuple-element.36), channel_id=1, source_target_pairs={{1,0},{2,1},{3,2},{4,3},{5,4},{6,5},{7,6},{9,8},{10,9},{11,10},{12... | collective-permute-start | bytes 147464 | tf_op jit(solution)/shard_map/ppermute | solution.py:336
  81.8 0.6 copy-start.8
  83.0 1.8 %copy-start.7 = (f32[1,128]{1,0:T(1,128)S(1)}, f32[1,128]{1,0:T(1,128)}, u32[]{:S(2)}) copy-start(f32[1,128]{1,0:T(1,128)} %get-tuple-element.28) | copy-start | bytes 1540
  83.0 2.3 %copy-start.1 = (f32[128,384]{1,0:T(8,128)S(1)}, f32[128,384]{1,0:T(8,128)}, u32[]{:S(2)}) copy-start(f32[128,384]{1,0:T(8,128)} %get-tuple-element.51) | copy-start | bytes 589828
  85.3 0.9 copy-start.3
  85.3 2.0 %copy-start = (f32[128,512]{1,0:T(8,128)S(1)}, f32[128,512]{1,0:T(8,128)}, u32[]{:S(2)}) copy-start(f32[128,512]{1,0:T(8,128)} %get-tuple-element.55) | copy-start | bytes 786436
  86.1 0.6 copy-start.6
  87.3 1.0 %copy-start.2 = (f32[256,128]{1,0:T(8,128)S(1)}, f32[256,128]{1,0:T(8,128)}, u32[]{:S(2)}) copy-start(f32[256,128]{1,0:T(8,128)} %get-tuple-element.56) | copy-start | bytes 393220

commit v2 on v1

v2 whole, which is shorter than its diff:
```python
import functools

import jax
import jax.numpy as jnp
from jax import lax
from jax.experimental import pallas as pl
from jax.experimental.pallas import tpu as pltpu
from jax.sharding import PartitionSpec as P

HEADS = 4
TRANS = 256
QWIN = 32
KWIN = 128
HALO = 48
EPSILON = 1e-05
CLIP_NORM = 256.0
BF = jnp.bfloat16
F32 = jnp.float32
LANES = 128
MESH = pl.DeviceIdType.MESH


def dot(a, b, dims=((1,), (0,))):
    return lax.dot_general(a, b, (dims, ((), ())), preferred_element_type=F32)


def dot_nt(a, b):
    return dot(a, b, ((1,), (1,)))


def dot_tn(a, b):
    return dot(a, b, ((0,), (0,)))


def stats(x):
    center = jnp.mean(x, axis=-1, keepdims=True)
    shifted = x - center
    rstd = lax.rsqrt(jnp.mean(shifted * shifted, axis=-1, keepdims=True) + EPSILON)
    return shifted * rstd, rstd


def norm_back(back, xhat, rstd, gain):
    scaled = back * gain
    first = jnp.mean(scaled, axis=-1, keepdims=True)
    second = jnp.mean(scaled * xhat, axis=-1, keepdims=True)
    return rstd * (scaled - first - xhat * second)


def split_hi_lo(row):
    hi = row.astype(BF)
    return hi, (row - hi.astype(F32)).astype(BF)


def mega_kernel(
    A, S,
    state_ref, cot_ref, qid_ref, again_ref, wp_ref, wo_ref, tb_ref, tgain_ref, wt_ref, wr_ref,
    out_ref, sg_ref, ga_ref, gb_ref,
    edge_ref, eid_ref, kid_ref, normed_ref, q_ref, kv_ref, p_ref, att_ref, batt_ref, bq_ref, bkv_ref,
    mask_ref, same_ref, acc_ref, row_ref, bnorm_ref, bres_ref, halo_ref, rim_ref,
    send_a, mid_a, in1_a, in2_a, all_a, send_b, mid_b, in1_b, in2_b, all_b,
    esend, erecv, hsend, hrecv, sems_a, sems_b,
):
    me_s, me_a = lax.axis_index("samp"), lax.axis_index("atom")
    samples, atoms, width = cot_ref.shape
    windows = atoms // QWIN
    near = -(-HALO // QWIN)
    hd = width // HEADS
    scale = 1.0 / (float(hd) ** 0.5)
    right, left = lax.rem(me_a + 1, A), lax.rem(me_a + A - 1, A)

    barrier = pltpu.get_barrier_semaphore()
    for d in range(1, A):
        pl.semaphore_signal(barrier, inc=1, device_id=(me_s, lax.rem(me_a + d, A)), device_id_type=MESH)
    for d in range(1, S):
        pl.semaphore_signal(barrier, inc=1, device_id=(lax.rem(me_s + d, S), me_a), device_id_type=MESH)

    def remote(src, dst, ss, rs, dev):
        return pltpu.make_async_remote_copy(
            src_ref=src, dst_ref=dst, send_sem=ss, recv_sem=rs, device_id=dev, device_id_type=MESH
        )

    rows_h = lax.broadcasted_iota(jnp.int32, (HEADS * QWIN, width), 0) // QWIN
    cols_h = lax.broadcasted_iota(jnp.int32, (HEADS * QWIN, width), 1) // hd
    head_f = (rows_h == cols_h).astype(F32)
    head_b = head_f.astype(BF)
    again = again_ref[...]
    tgain = tgain_ref[...]
    lane_head = lax.broadcasted_iota(jnp.int32, (1, LANES), 1) // QWIN
    bias_row = jnp.zeros((1, LANES), F32)
    for h in range(HEADS):
        bias_row = jnp.where(lane_head == h, tb_ref[h], bias_row)

    acc_ref[...] = jnp.zeros_like(acc_ref)
    row_ref[...] = jnp.zeros_like(row_ref)
    bkv_ref[...] = jnp.zeros_like(bkv_ref)

    def project(s, _):
        xhat, _r = stats(state_ref[s].astype(F32))
        normed = (xhat * again).astype(BF)
        normed_ref[s, HALO : HALO + atoms] = normed
        both = dot(normed, wp_ref[...]).astype(BF)
        q_ref[s] = both[:, :width]
        kv_ref[s, HALO : HALO + atoms] = both[:, width:]
        return 0

    lax.fori_loop(0, samples, project, 0)

    pl.semaphore_wait(barrier, A + S - 2)
    edges = [
        remote(state_ref.at[:, pl.ds(atoms - HALO, HALO), :], edge_ref.at[0], esend.at[0], erecv.at[0], (me_s, right)),
        remote(state_ref.at[:, pl.ds(0, HALO), :], edge_ref.at[1], esend.at[1], erecv.at[1], (me_s, left)),
        remote(qid_ref.at[pl.ds(windows - near, near)], eid_ref.at[0], esend.at[2], erecv.at[2], (me_s, right)),
        remote(qid_ref.at[pl.ds(0, near)], eid_ref.at[1], esend.at[3], erecv.at[3], (me_s, left)),
    ]
    for copy in edges:
        copy.start()

    def columns(rows):
        count = rows.shape[0]
        full = jnp.concatenate([rows.astype(F32), jnp.zeros((LANES - count, LANES), F32)], axis=0)
        turned = full.T
        return [jnp.broadcast_to(turned[:QWIN, j : j + 1], (QWIN, LANES)) for j in range(count)]

    for j, column in enumerate(columns(qid_ref[:, 0, :])):
        kid_ref[HALO + j * QWIN : HALO + (j + 1) * QWIN, :] = column

    def masks(w):
        base = pl.multiple_of(w * QWIN, QWIN)
        kid = kid_ref[pl.ds(base, KWIN), :]
        same = (kid == qid_ref[w][0:1].astype(F32)).astype(F32)
        same_ref[w] = same
        mask = jnp.where(kid > 0.0, same * bias_row, -1e30)
        mask_ref[w] = mask
        return mask

    def spread(rows):
        return jnp.concatenate([rows] * HEADS, axis=0) * head_b

    def gather_heads(value):
        return jnp.sum((value * head_f).reshape(HEADS, QWIN, width), axis=0)

    def attend_at(w):
        base = pl.multiple_of(w * QWIN, QWIN)
        mask = masks(w)
        for s in range(samples):
            keys = kv_ref[s, pl.ds(base, KWIN), :width]
            vals = kv_ref[s, pl.ds(base, KWIN), width:]
            score = dot_nt(keys, spread(q_ref[s, pl.ds(base, QWIN), :])) * scale + mask
            weight = jnp.exp(score - jnp.max(score, axis=0, keepdims=True))
            prob = (weight * (1.0 / jnp.sum(weight, axis=0, keepdims=True))).astype(BF)
            p_ref[s, w] = prob
            att_ref[s, pl.ds(base, QWIN), :] = gather_heads(dot_tn(prob, vals)).astype(BF)

    def attend(w, _):
        attend_at(w)
        return 0

    lax.fori_loop(near, windows - near, attend, 0)

    for copy in edges:
        copy.wait()
    has_before = (me_a > 0).astype(F32)
    has_after = (me_a < A - 1).astype(F32)
    for side, has in ((0, has_before), (1, has_after)):
        cols = jnp.concatenate(columns(eid_ref[side, :, 0, :]), axis=0) * has
        if side == 0:
            kid_ref[:HALO, :] = cols[near * QWIN - HALO :]
        else:
            kid_ref[HALO + atoms :, :] = cols[:HALO]

    def project_edge(s, _):
        both_edges = jnp.concatenate([edge_ref[0, s], edge_ref[1, s]], axis=0)
        xhat, _r = stats(both_edges.astype(F32))
        normed = (xhat * again).astype(BF)
        normed_ref[s, :HALO] = normed[:HALO]
        normed_ref[s, HALO + atoms :] = normed[HALO:]
        both = dot(normed, wp_ref[:, width:]).astype(BF)
        kv_ref[s, :HALO] = both[:HALO]
        kv_ref[s, HALO + atoms :] = both[HALO:]
        return 0

    lax.fori_loop(0, samples, project_edge, 0)

    def attend_edge(i, _):
        attend_at(jnp.where(i < near, i, windows - 2 * near + i))
        return 0

    lax.fori_loop(0, 2 * near, attend_edge, 0)

    def transit(s, _):
        state = state_ref[s].astype(F32)
        att = att_ref[s]
        residual = (state + dot(att, wo_ref[...])).astype(BF).astype(F32)
        xhat, rstd = stats(residual)
        tin = (xhat * tgain).astype(BF)
        both = dot(tin, wt_ref[...])
        gate, up = both[:, :TRANS], both[:, TRANS:]
        sig = 1.0 / (1.0 + jnp.exp(-gate))
        silu = gate * sig
        gated = (silu * up).astype(BF)
        out_ref[s] = (residual + dot(gated, wr_ref[...])).astype(BF)
        cot = cot_ref[s]
        acc_ref[5:7] += dot_tn(gated, cot).reshape(2, LANES, LANES)
        bg = dot_nt(cot, wr_ref[...])
        back_gate = (bg * up * sig * (1.0 + gate * (1.0 - sig))).astype(BF)
        back_up = (bg * silu).astype(BF)
        bh = jnp.concatenate([back_gate, back_up], axis=1)
        gt = dot_tn(tin, bh)
        for j in range(4):
            acc_ref[1 + j] += gt[:, j * LANES : (j + 1) * LANES]
        bt = dot_nt(bh, wt_ref[...])
        row_ref[1:2] += jnp.sum(bt * xhat, axis=0, keepdims=True)
        bres = cot.astype(F32) + norm_back(bt, xhat, rstd, tgain)
        bres_ref[s] = bres
        b16 = bres.astype(BF)
        acc_ref[0] += dot_tn(att, b16)
        batt_ref[s] = dot_nt(b16, wo_ref[...]).astype(BF)
        return 0

    lax.fori_loop(0, samples, transit, 0)

    class Reduce:
        def __init__(self, send, in1, mid, in2, full, sems):
            self.send, self.in1, self.mid, self.in2, self.full, self.sems = send, in1, mid, in2, full, sems
            self.started = []

        def over_atom(self, src_of, dst_of, k):
            copies = []
            for d in range(1, A):
                peer = lax.rem(me_a + d, A)
                copy = remote(src_of(peer), dst_of(d), self.sems.at[k, 0, d - 1], self.sems.at[k, 1, d - 1], (me_s, peer))
                copy.start()
                copies.append(copy)
            self.started += copies
            return copies

        def over_samp(self, src_of, dst_of, k):
            copies = []
            for d in range(1, S):
                peer = lax.rem(me_s + d, S)
                copy = remote(src_of(peer), dst_of(d), self.sems.at[k, 0, d - 1], self.sems.at[k, 1, d - 1], (peer, me_a))
                copy.start()
                copies.append(copy)
            self.started += copies
            return copies

        def step1(self):
            self.c1 = self.over_atom(lambda p: self.send.at[p], lambda d: self.in1.at[d - 1], 0)

        def step2(self):
            total = self.send[me_a].astype(F32)
            for d in range(1, A):
                self.c1[d - 1].wait_recv()
                total = total + self.in1[d - 1].astype(F32)
            self.mid[...] = total.astype(BF)
            self.c2 = self.over_samp(lambda p: self.mid.at[p], lambda d: self.in2.at[d - 1], 1)

        def step3(self):
            mine = self.mid[me_s].astype(F32)
            for d in range(1, S):
                self.c2[d - 1].wait_recv()
                mine = mine + self.in2[d - 1].astype(F32)
            self.full[me_a, me_s] = mine.astype(BF)
            self.over_samp(lambda p: self.full.at[me_a, me_s], lambda d: self.full.at[me_a, me_s], 2)

        def step4(self):
            for d in range(1, S):
                src = lax.rem(me_s + S - d, S)
                ref = self.full.at[me_a, src]
                remote(ref, ref, self.sems.at[2, 0, d - 1], self.sems.at[2, 1, d - 1], (src, me_a)).wait_recv()
            self.over_atom(lambda p: self.full.at[me_a], lambda d: self.full.at[me_a], 3)

        def step5(self):
            for d in range(1, A):
                src = lax.rem(me_a + A - d, A)
                ref = self.full.at[src]
                remote(ref, ref, self.sems.at[3, 0, d - 1], self.sems.at[3, 1, d - 1], (me_s, src)).wait_recv()
            for copy in self.started:
                copy.wait_send()

    def pack(dst, parts):
        rows = A * S * dst.shape[2]
        used = sum(p.shape[0] for p in parts)
        if rows > used:
            parts = parts + [jnp.zeros((rows - used, LANES), F32)]
        dst[...] = jnp.concatenate(parts, axis=0).reshape(dst.shape).astype(BF)

    red_a = Reduce(send_a, in1_a, mid_a, in2_a, all_a, sems_a)
    red_b = Reduce(send_b, in1_b, mid_b, in2_b, all_b, sems_b)

    pack(send_a, [acc_ref[j] for j in range(7)])
    red_a.step1()

    def attend_back(w, _):
        base = pl.multiple_of(w * QWIN, QWIN)
        total = jnp.zeros((KWIN, LANES), F32)
        for s in range(samples):
            keys = kv_ref[s, pl.ds(base, KWIN), :width]
            vals = kv_ref[s, pl.ds(base, KWIN), width:]
            qs = spread(q_ref[s, pl.ds(base, QWIN), :])
            bo = spread(batt_ref[s, pl.ds(base, QWIN), :])
            prob = p_ref[s, w]
            pf = prob.astype(F32)
            bp = dot_nt(vals, bo)
            pbp = pf * bp
            bs = pbp - pf * jnp.sum(pbp, axis=0, keepdims=True)
            total = total + bs
            b16 = (bs * scale).astype(BF)
            bq_ref[s, pl.ds(base, QWIN), :] = gather_heads(dot_tn(b16, keys)).astype(BF)
            bkv_ref[s, pl.ds(base, KWIN), :width] += dot(b16, qs)
            bkv_ref[s, pl.ds(base, KWIN), width:] += dot(prob, bo)
        row_ref[2:3] += jnp.sum(total * same_ref[w], axis=0, keepdims=True)
        return 0

    half = windows // 2
    lax.fori_loop(0, half, attend_back, 0)
    red_a.step2()
    lax.fori_loop(half, windows, attend_back, 0)
    red_a.step3()

    def finish(s, _):
        normed = normed_ref[s]
        bkv = bkv_ref[s].astype(BF)
        bq = bq_ref[s]
        acc_ref[7] += dot_tn(normed[HALO : HALO + atoms], bq)
        gkv = dot_tn(normed, bkv)
        acc_ref[8] += gkv[:, :LANES]
        acc_ref[9] += gkv[:, LANES:]
        back = dot_nt(bkv, wp_ref[:, width:])
        own = back[HALO : HALO + atoms] + dot_nt(bq, wp_ref[:, :width])
        xhat, _r = stats(state_ref[s].astype(F32))
        xb, _r = stats(edge_ref[0, s].astype(F32))
        xa, _r = stats(edge_ref[1, s].astype(F32))
        halo_before = back[:HALO]
        halo_after = back[HALO + atoms :]
        row_ref[0:1] += (
            jnp.sum(own * xhat, axis=0, keepdims=True)
            + jnp.sum(halo_before * xb, axis=0, keepdims=True)
            + jnp.sum(halo_after * xa, axis=0, keepdims=True)
        )
        halo_ref[0, s] = halo_after.astype(BF)
        halo_ref[1, s] = halo_before.astype(BF)
        bnorm_ref[s] = own
        return 0

    lax.fori_loop(0, samples, finish, 0)

    pieces = [acc_ref[7 + j] for j in range(3)]
    for i in range(3):
        hi, lo = split_hi_lo(row_ref[i : i + 1])
        pieces += [hi.astype(F32), lo.astype(F32)]
    pieces[3:] = [jnp.concatenate(pieces[3:] + [jnp.zeros((10, LANES), F32)], axis=0)]
    pack(send_b, pieces)
    red_b.step1()
    rims = [
        remote(halo_ref.at[0], rim_ref.at[0], hsend.at[0], hrecv.at[0], (me_s, right)),
        remote(halo_ref.at[1], rim_ref.at[1], hsend.at[1], hrecv.at[1], (me_s, left)),
    ]
    for copy in rims:
        copy.start()
    red_a.step4()
    red_b.step2()
    for copy in rims:
        copy.wait()

    def close(s, _):
        xhat, rstd = stats(state_ref[s].astype(F32))
        own = bnorm_ref[s]
        top = own[:HALO] + rim_ref[0, s].astype(F32) * has_before
        bottom = own[atoms - HALO :] + rim_ref[1, s].astype(F32) * has_after
        back = jnp.concatenate([top, own[HALO : atoms - HALO], bottom], axis=0)
        sg_ref[s] = (bres_ref[s] + norm_back(back, xhat, rstd, again)).astype(BF)
        return 0

    lax.fori_loop(0, samples // 2, close, 0)
    red_b.step3()
    lax.fori_loop(samples // 2, samples, close, 0)
    red_b.step4()
    red_a.step5()
    ga_ref[...] = all_a[...]
    red_b.step5()
    gb_ref[...] = all_b[...]


def clip_kernel(ga_ref, gb_ref, out_in, sg_in, out_ref, sg_ref, gag_ref, gp_ref, go_ref, gb_out, gtg_ref, gt_ref, gr_ref):
    out_ref[...] = out_in[...]
    sg_ref[...] = sg_in[...]
    fa = ga_ref[...].astype(F32).reshape(-1, LANES)
    fb = gb_ref[...].astype(F32).reshape(-1, LANES)
    blocks = [fa[j * LANES : (j + 1) * LANES] for j in range(7)] + [fb[j * LANES : (j + 1) * LANES] for j in range(3)]
    rest = fb[3 * LANES : 3 * LANES + 6]
    rows = [rest[0:1] + rest[1:2], rest[2:3] + rest[3:4], rest[4:5] + rest[5:6]]
    lane = lax.broadcasted_iota(jnp.int32, (1, LANES), 1)
    bias = jnp.zeros((1, LANES), F32)
    for h in range(HEADS):
        part = jnp.sum(jnp.where(lane // QWIN == h, rows[2], 0.0), axis=1, keepdims=True)
        bias = bias + jnp.where(lane == h, part, 0.0)
    sq = blocks[0] * blocks[0]
    for b in blocks[1:]:
        sq = sq + b * b
    sq = jnp.sum(sq, axis=0, keepdims=True) + rows[0] * rows[0] + rows[1] * rows[1] + bias * bias
    squares = jnp.sum(sq, axis=1, keepdims=True)
    factor = CLIP_NORM / jnp.sqrt(squares + CLIP_NORM * CLIP_NORM)
    gag_ref[...] = rows[0] * factor
    gtg_ref[...] = rows[1] * factor
    gb_out[...] = bias * factor
    go_ref[...] = blocks[0] * factor
    for j in range(4):
        gt_ref[:, j * LANES : (j + 1) * LANES] = blocks[1 + j] * factor
    for j in range(2):
        gr_ref[j * LANES : (j + 1) * LANES, :] = blocks[5 + j] * factor
    for j in range(3):
        gp_ref[:, j * LANES : (j + 1) * LANES] = blocks[7 + j] * factor


def on_device(A, S, atom_state, atom_token, window_valid, attend_gain, project_weight, output_weight,
              token_bias, transit_gain, transit_weight, return_weight, cotangent):
    samples, atoms, width = atom_state.shape
    windows = window_valid.shape[0]
    ext = atoms + 2 * HALO
    near = -(-HALO // QWIN)
    slots = lax.broadcasted_iota(jnp.int32, (windows, QWIN), 1)
    ids = jnp.where(slots < window_valid[:, None], atom_token.reshape(windows, QWIN) + 1, 0)
    qid = jnp.broadcast_to(jnp.tile(ids, (1, HEADS))[:, None, :], (windows, 8, LANES))
    again = attend_gain.reshape(1, width)
    tgain = transit_gain.reshape(1, width)
    shards = A * S
    per_a = -(-7 * LANES // (shards * 16)) * 16
    per_b = -(-(3 * LANES + 16) // (shards * 16)) * 16
    vm = pl.BlockSpec(memory_space=pltpu.VMEM)
    sds = jax.ShapeDtypeStruct
    act = (samples, atoms, width)
    dma = pltpu.SemaphoreType.DMA
    top = max(A, S) - 1

    def buffers(per):
        return [
            pltpu.VMEM((A, S, per, LANES), BF),
            pltpu.VMEM((S, per, LANES), BF),
            pltpu.VMEM((A - 1, S, per, LANES), BF),
            pltpu.VMEM((S - 1, per, LANES), BF),
            pltpu.VMEM((A, S, per, LANES), BF),
        ]

    block_out, sg, ga, gb = pl.pallas_call(
        functools.partial(mega_kernel, A, S),
        out_shape=(sds(act, BF), sds(act, BF), sds((A, S, per_a, LANES), BF), sds((A, S, per_b, LANES), BF)),
        in_specs=[vm] * 6 + [pl.BlockSpec(memory_space=pltpu.SMEM)] + [vm] * 3,
        out_specs=(vm,) * 4,
        scratch_shapes=[
            pltpu.VMEM((2, samples, HALO, width), BF),
            pltpu.VMEM((2, near, 8, LANES), jnp.int32),
            pltpu.VMEM((ext, LANES), F32),
            pltpu.VMEM((samples, ext, width), BF),
            pltpu.VMEM(act, BF),
            pltpu.VMEM((samples, ext, 2 * width), BF),
            pltpu.VMEM((samples, windows, KWIN, LANES), BF),
            pltpu.VMEM(act, BF),
            pltpu.VMEM(act, BF),
            pltpu.VMEM(act, BF),
            pltpu.VMEM((samples, ext, 2 * width), F32),
            pltpu.VMEM((windows, KWIN, LANES), F32),
            pltpu.VMEM((windows, KWIN, LANES), F32),
            pltpu.VMEM((10, LANES, LANES), F32),
            pltpu.VMEM((8, LANES), F32),
            pltpu.VMEM(act, F32),
            pltpu.VMEM(act, F32),
            pltpu.VMEM((2, samples, HALO, width), BF),
            pltpu.VMEM((2, samples, HALO, width), BF),
        ]
        + buffers(per_a)
        + buffers(per_b)
        + [dma((4,)), dma((4,)), dma((2,)), dma((2,)), dma((4, 2, top)), dma((4, 2, top))],
        compiler_params=pltpu.CompilerParams(collective_id=0, has_side_effects=True),
        name="block",
    )(atom_state, cotangent, qid, again, project_weight, output_weight, token_bias, tgain,
      transit_weight, return_weight)
    block_out, sg, gag, gp, go, gbias, gtg, gt, gr = pl.pallas_call(
        clip_kernel,
        out_shape=(sds(act, BF), sds(act, BF), sds((1, width), F32), sds((width, 3 * width), F32),
                   sds((width, width), F32), sds((1, LANES), F32), sds((1, width), F32),
                   sds((width, 2 * TRANS), F32), sds((TRANS, width), F32)),
        in_specs=[vm] * 4,
        out_specs=(vm,) * 9,
        name="clip",
    )(ga, gb, block_out, sg)
    return (block_out, sg, gag.reshape(width), gp, go, gbias[0, :HEADS], gtg.reshape(width), gt, gr)


def solution(mesh):
    A, S = mesh.shape["atom"], mesh.shape["samp"]
    act = P("samp", "atom", None)
    return jax.shard_map(
        functools.partial(on_device, A, S),
        mesh=mesh,
        in_specs=(act, P("atom"), P("atom"), P(), P(), P(), P(), P(), P(), P(), act),
        out_specs=(act, act, P(), P(), P(), P(), P(), P(), P()),
        check_vma=False,
    )
```

time: 89.4 us -> 62.2 us (0.70)
  starting transfers between devices: 10.1 us -> 0 us
  local copies, waits for them, and re-layouts: 10.3 us -> 3.21 us
  Pallas kernels: 63.7 us -> 58.1 us
  other arithmetic: 2.59 us -> 0.07 us
  waiting for transfers between devices: 1.55 us -> 0 us
    ppermute x4 -> x0, starting transfers between devices: 10.1 us -> none  [the longest x1 5.12 us: on_device(): before = lax.ppermute(atom_state[:, atoms - HALO:], 'atom', up_pairs)]
    pallas_call x2, Pallas kernels: 63.7 us -> 58.1 us  [the longest x1 55.7 us: on_device(): pl.pallas_call(functools.partial(mega_kernel, A, S), out_shape=(sds(act,...]
    unnamed x25 -> x6, local copies, waits for them, and re-layouts: 6.58 us -> 1.91 us
    concatenate x2 -> x0, other arithmetic: 1.85 us -> none  [the longest x1 1.77 us: on_device(): ext_state = jnp.concatenate([before, atom_state, after], axis=1)]
    ppermute x4 -> x0, waiting for transfers between devices: 1.55 us -> none  [the longest x1 1.54 us: on_device(): after = lax.ppermute(atom_state[:, :HALO], 'atom', down_pairs)]
    another operation x4 -> x2, local copies, waits for them, and re-layouts: 1.36 us -> 0.09 us  [on_device(): jnp.tile(ids, (1, HEADS))[:, None, :]]
    slice x2 -> x0, local copies, waits for them, and re-layouts: 0.91 us -> none  [the longest x1 0.84 us: on_device(): before = lax.ppermute(atom_state[:, atoms - HALO:], 'atom', up_pairs)]
  transfers between devices with their start and end apart: 4 -> 0, of which waited for: 1 -> 0; matrix products, arithmetic and copies ran while one was open for 3% -> 0% of each run, Pallas kernels for 0% -> 0%
where the time goes in v2:
time: 62.2 us; the launch traced here: 62 us
  Pallas kernels  58.1 us (93%)
  local copies, waits for them, and re-layouts  3.21 us (5%)
  between operations  0.66 us (1%)
    pallas_call x1, Pallas kernels, on_device(): pl.pallas_call(functools.partial(mega_kernel, A, S), out_shape=(sds(act,...  55.7 us
    pallas_call x1, Pallas kernels, on_device(): pl.pallas_call(clip_kernel, out_shape=(sds(act, BF), sds(act, BF), sds((1...  2.37 us
    unnamed x6, local copies, waits for them, and re-layouts  1.91 us

profile of v2, /device:TPU:0, one launch (start us, length us, event | category | flops | bytes accessed | tf_op | source)
XLA Modules:
  0.0 62.0 jit_solution(13112550550644123122)
XLA Ops:
  0.6 0.0 copy-start
  0.7 0.7 %copy-done = s32[320]{0:T(512)S(1)} copy-done((s32[320]{0:T(512)S(1)}, s32[320]{0:T(512)}, u32[]{:S(2)}) %copy-start) | copy-done | bytes 1304
  1.3 0.0 copy-start.1
  1.3 0.1 add.15
  1.4 0.6 copy-done.1
  2.0 0.1 fusion
  2.1 0.1 tile.9
  2.1 0.6 %broadcast_in_dim.11.qid_ref = s32[10,8,128]{2,1,0:T(8,128)} broadcast(s32[10,128]{1,0:T(8,128)S(1)} %tile.9), dimensions={0,2} | broadcast | bytes 46080 | tf_op jit(solution)/shard_map/broadcast_in_dim | solution.py:424
  2.8 55.7 %block.1 = (bf16[4,320,128]{2,1,0:T(8,128)(2,1)}, bf16[4,320,128]{2,1,0:T(8,128)(2,1)}, bf16[8,4,32,128]{3,2,1,0:T(8,128)(2,1)}, bf16[8,4,16,128]{3,2,1,0:T(8,128)(2,1)}) custom-call(bf16[4,320,128]{2,1,0:T(8,128)(2,1)} %state_ref.1, bf16[4,320,128]{2,1,0:T(8,128)(2,1)} %cot_ref.1, s32[10,8,128]{2,1,0:T(8,128)} %broadcast_in_dim.11.qid_ref, ...), custom_call_target="tpu_custom_call" | custom-call | tf_op jit(solution)/shard_map/block/pallas_call | solution.py:445
  58.5 2.4 %clip.1 = (bf16[4,320,128]{2,1,0:T(8,128)(2,1)}, bf16[4,320,128]{2,1,0:T(8,128)(2,1)}, f32[1,128]{1,0:T(1,128)}, f32[128,384]{1,0:T(8,128)}, f32[128,128]{1,0:T(...) custom-call(bf16[8,4,32,128]{3,2,1,0:T(8,128)(2,1)} %get-tuple-element.22.ga_ref, ...), custom_call_target="tpu_custom_call" | custom-call | tf_op jit(solution)/shard_map/clip/pallas_call | solution.py:478
  60.8 0.0 copy-start.2
  60.8 0.7 %copy-done.2 = f32[1,128]{1,0:T(1,128)S(1)} copy-done((f32[1,128]{1,0:T(1,128)S(1)}, f32[1,128]{1,0:T(1,128)}, u32[]{:S(2)}) %copy-start.2) | copy-done | bytes 536
  61.5 0.5 slice_bitcast_fusion
  (2 shorter events, 0.0 us)
Async XLA Ops:
  0.6 0.7 %copy-start = (s32[320]{0:T(512)S(1)}, s32[320]{0:T(512)}, u32[]{:S(2)}) copy-start(s32[320]{0:T(512)} %param.12) | copy-start | bytes 3844
  1.3 0.7 %copy-start.1 = (s32[10]{0:T(128)S(1)}, s32[10]{0:T(128)}, u32[]{:S(2)}) copy-start(s32[10]{0:T(128)} %param.13) | copy-start | bytes 124
  60.8 0.7 %copy-start.2 = (f32[1,128]{1,0:T(1,128)S(1)}, f32[1,128]{1,0:T(1,128)}, u32[]{:S(2)}) copy-start(f32[1,128]{1,0:T(1,128)} %get-tuple-element.31) | copy-start | bytes 1540

commit v3 on v2

--- a/solution.py
+++ b/solution.py
@@ -58,7 +58,7 @@
     edge_ref, eid_ref, kid_ref, normed_ref, q_ref, kv_ref, p_ref, att_ref, batt_ref, bq_ref, bkv_ref,
     mask_ref, same_ref, acc_ref, row_ref, bnorm_ref, bres_ref, halo_ref, rim_ref,
     send_a, mid_a, in1_a, in2_a, all_a, send_b, mid_b, in1_b, in2_b, all_b,
-    esend, erecv, hsend, hrecv, sems_a, sems_b,
+    esend, erecv, hsend, hrecv, sems_a, sems_b, turn_ref,
 ):
     me_s, me_a = lax.axis_index("samp"), lax.axis_index("atom")
     samples, atoms, width = cot_ref.shape
@@ -145,7 +145,8 @@
         for s in range(samples):
             keys = kv_ref[s, pl.ds(base, KWIN), :width]
             vals = kv_ref[s, pl.ds(base, KWIN), width:]
-            score = dot_nt(keys, spread(q_ref[s, pl.ds(base, QWIN), :])) * scale + mask
+            turn_ref[s] = spread(q_ref[s, pl.ds(base, QWIN), :]).T
+            score = dot(keys, turn_ref[s]) * scale + mask
             weight = jnp.exp(score - jnp.max(score, axis=0, keepdims=True))
             prob = (weight * (1.0 / jnp.sum(weight, axis=0, keepdims=True))).astype(BF)
             p_ref[s, w] = prob
@@ -301,7 +302,8 @@
             bo = spread(batt_ref[s, pl.ds(base, QWIN), :])
             prob = p_ref[s, w]
             pf = prob.astype(F32)
-            bp = dot_nt(vals, bo)
+            turn_ref[s] = bo.T
+            bp = dot(vals, turn_ref[s])
             pbp = pf * bp
             bs = pbp - pf * jnp.sum(pbp, axis=0, keepdims=True)
             total = total + bs
@@ -470,7 +472,8 @@
         ]
         + buffers(per_a)
         + buffers(per_b)
-        + [dma((4,)), dma((4,)), dma((2,)), dma((2,)), dma((4, 2, top)), dma((4, 2, top))],
+        + [dma((4,)), dma((4,)), dma((2,)), dma((2,)), dma((4, 2, top)), dma((4, 2, top)),
+           pltpu.VMEM((samples, HEADS * QWIN, LANES), BF)],
         compiler_params=pltpu.CompilerParams(collective_id=0, has_side_effects=True),
         name="block",
     )(atom_state, cotangent, qid, again, project_weight, output_weight, token_bias, tgain,

time: 62.2 us -> 53.1 us (0.85)
  Pallas kernels: 58.1 us -> 49 us
    pallas_call x1, Pallas kernels: 55.7 us -> 46.6 us  [on_device(): pl.pallas_call(functools.partial(mega_kernel, A, S), out_shape=(sds(act,...]
where the time goes in v3:
time: 53.1 us; the launch traced here: 52.9 us
  Pallas kernels  49 us (92%)
  local copies, waits for them, and re-layouts  3.21 us (6%)
  between operations  0.66 us (1%)
    pallas_call x1, Pallas kernels, on_device(): pl.pallas_call(functools.partial(mega_kernel, A, S), out_shape=(sds(act,...  46.6 us
    pallas_call x1, Pallas kernels, on_device(): pl.pallas_call(clip_kernel, out_shape=(sds(act, BF), sds(act, BF), sds((1...  2.37 us
    unnamed x6, local copies, waits for them, and re-layouts  1.91 us

profile of v3, /device:TPU:0, one launch (start us, length us, event | category | flops | bytes accessed | tf_op | source)
XLA Modules:
  0.0 52.9 jit_solution(12232887743220509389)
XLA Ops:
  0.6 0.0 copy-start
  0.7 0.7 %copy-done = s32[320]{0:T(512)S(1)} copy-done((s32[320]{0:T(512)S(1)}, s32[320]{0:T(512)}, u32[]{:S(2)}) %copy-start) | copy-done | bytes 1304
  1.3 0.0 copy-start.1
  1.3 0.1 add.15
  1.4 0.6 %copy-done.1 = s32[10]{0:T(128)S(1)} copy-done((s32[10]{0:T(128)S(1)}, s32[10]{0:T(128)}, u32[]{:S(2)}) %copy-start.1) | copy-done | bytes 64
  2.0 0.1 fusion
  2.1 0.1 tile.9
  2.1 0.6 %broadcast_in_dim.11.qid_ref = s32[10,8,128]{2,1,0:T(8,128)} broadcast(s32[10,128]{1,0:T(8,128)S(1)} %tile.9), dimensions={0,2} | broadcast | bytes 46080 | tf_op jit(solution)/shard_map/broadcast_in_dim | solution.py:426
  2.8 46.6 %block.1 = (bf16[4,320,128]{2,1,0:T(8,128)(2,1)}, bf16[4,320,128]{2,1,0:T(8,128)(2,1)}, bf16[8,4,32,128]{3,2,1,0:T(8,128)(2,1)}, bf16[8,4,16,128]{3,2,1,0:T(8,128)(2,1)}) custom-call(bf16[4,320,128]{2,1,0:T(8,128)(2,1)} %state_ref.1, bf16[4,320,128]{2,1,0:T(8,128)(2,1)} %cot_ref.1, s32[10,8,128]{2,1,0:T(8,128)} %broadcast_in_dim.11.qid_ref, ...), custom_call_target="tpu_custom_call" | custom-call | tf_op jit(solution)/shard_map/block/pallas_call | solution.py:447
  49.4 2.4 %clip.1 = (bf16[4,320,128]{2,1,0:T(8,128)(2,1)}, bf16[4,320,128]{2,1,0:T(8,128)(2,1)}, f32[1,128]{1,0:T(1,128)}, f32[128,384]{1,0:T(8,128)}, f32[128,128]{1,0:T(...) custom-call(bf16[8,4,32,128]{3,2,1,0:T(8,128)(2,1)} %get-tuple-element.22.ga_ref, ...), custom_call_target="tpu_custom_call" | custom-call | tf_op jit(solution)/shard_map/clip/pallas_call | solution.py:481
  51.8 0.0 copy-start.2
  51.8 0.7 %copy-done.2 = f32[1,128]{1,0:T(1,128)S(1)} copy-done((f32[1,128]{1,0:T(1,128)S(1)}, f32[1,128]{1,0:T(1,128)}, u32[]{:S(2)}) %copy-start.2) | copy-done | bytes 536
  52.4 0.5 slice_bitcast_fusion
  (2 shorter events, 0.0 us)
Async XLA Ops:
  0.6 0.7 %copy-start = (s32[320]{0:T(512)S(1)}, s32[320]{0:T(512)}, u32[]{:S(2)}) copy-start(s32[320]{0:T(512)} %param.12) | copy-start | bytes 3844
  1.3 0.7 %copy-start.1 = (s32[10]{0:T(128)S(1)}, s32[10]{0:T(128)}, u32[]{:S(2)}) copy-start(s32[10]{0:T(128)} %param.13) | copy-start | bytes 124
  51.8 0.7 %copy-start.2 = (f32[1,128]{1,0:T(1,128)S(1)}, f32[1,128]{1,0:T(1,128)}, u32[]{:S(2)}) copy-start(f32[1,128]{1,0:T(1,128)} %get-tuple-element.31) | copy-start | bytes 1540
